TPU v7x, 32 devices: a whole 2x2x4 slice. The times are simulated.
32 devices in a mesh: sub: 8 (over z, y), inner: 4 (over x, core).
Axes of the slice: x: 2, y: 2, z: 4, core: 2. Of those that a mesh axis runs over, the one named last changes fastest.
Arguments:
- solution: float32 [32, 3, 32, 16, 128], P(None, None, 'sub', 'inner'), may hold values from -6 to 6
- residual: float32 [32, 3, 32, 16, 128], P(None, None, 'sub', 'inner'), may hold values from -6 to 6
- direction: float32 [32, 3, 32, 16, 128], P(None, None, 'sub', 'inner'), may hold values from -6 to 6
- mass: float32 [32, 16, 128], P('sub', 'inner'), may hold values from 0.2 to 5
- coarse_basis: float32 [32, 3, 32, 16, 128], P(None, None, 'sub', 'inner'), may hold values from -1 to 1
- line_inverse: float32 [8, 4, 128, 128], P('sub', 'inner'), may hold values from -1.5 to 1.5
- coarse_factor: float32 [1024, 1024], P(('sub', 'inner')), may hold values from -1 to 1
Outputs:
- new_solution: float32 [32, 3, 32, 16, 128], P(None, None, 'sub', 'inner')
- new_residual: float32 [32, 3, 32, 16, 128], P(None, None, 'sub', 'inner')
- new_direction: float32 [32, 3, 32, 16, 128], P(None, None, 'sub', 'inner')
All inputs are finite; a program needn't handle non-finite values.
Results may differ from a plain program's by a relative error of at most 0.00017.
Values sent between devices are 32-bit elements; how exact they have to be, the bound alone decides.
A program may use at most 64 MiB of HBM per device.

v0:
```python
import jax
import jax.numpy as jnp
from jax import lax
from jax.sharding import PartitionSpec as P

exact_mode = lax.Precision.HIGHEST


def with_halo(array, sides, width):
    for axis, dim in sides:
        count, length = (lax.axis_size(axis), array.shape[dim])
        up = [(i, (i + 1) % count) for i in range(count - 1)]
        down = [(j, i) for i, j in up]
        last = lax.slice_in_dim(array, length - width, length, axis=dim)
        initial = lax.slice_in_dim(array, 0, width, axis=dim)
        before = lax.ppermute(last, axis, up)
        after = lax.ppermute(initial, axis, down)
        array = jnp.concatenate([before, array, after], axis=dim)
    return array


def shifted(padded, which, offset):
    window = [slice(None), slice(None)]
    for place in (2, 3, 4):
        length = padded.shape[place]
        if place == which:
            window.append(slice(2 + offset, length - 2 + offset))
        else:
            window.append(slice(2, length - 2))
    return padded[tuple(window)]


def operate(direction, mass):
    widened = with_halo(direction, (("sub", 2), ("inner", 3)), 2)
    padded = jnp.pad(widened, ((0, 0), (0, 0), (0, 0), (0, 0), (2, 2)))
    center = shifted(padded, 2, 0)
    nearby = jnp.zeros_like(center)
    farther = jnp.zeros_like(center)
    for which in (2, 3, 4):
        nearby = nearby + shifted(padded, which, 1) + shifted(padded, which, -1)
        farther = farther + shifted(padded, which, 2) + shifted(padded, which, -2)
    return (mass + 7.5) * center - 4.0 / 3.0 * nearby + 1.0 / 12.0 * farther


def spd_solve(lower, rhs):
    middle = lax.linalg.triangular_solve(lower, rhs, left_side=True, lower=True)
    return lax.linalg.triangular_solve(lower, middle, left_side=True, lower=True, transpose_a=True)


def along_lines(flat, inverse):
    lines = flat.reshape(-1, inverse.shape[0])
    return jnp.dot(lines, inverse.T, precision=exact_mode).reshape(flat.shape)


def product(left, right):
    return jnp.dot(left, right.T, precision=exact_mode)


def on_device(solution, residual, direction, mass, coarse_basis, line_inverse, coarse_factor):
    directions = direction.shape[0]
    shape = direction.shape
    inverse = line_inverse[0, 0]
    image = operate(direction, mass)
    flat_p = direction.reshape(directions, -1)
    flat_q = image.reshape(directions, -1)
    flat_r = residual.reshape(directions, -1)
    flat_s = solution.reshape(directions, -1)
    basis_flat = coarse_basis.reshape(coarse_basis.shape[0], -1)
    lined_r = along_lines(flat_r, inverse)
    lined_q = along_lines(flat_q, inverse)
    rhs_r = product(basis_flat, flat_r)
    rhs_q = product(basis_flat, flat_q)
    summed = lax.psum(
        (
            product(flat_p, flat_q),
            product(flat_p, flat_r),
            product(flat_q, lined_r),
            product(flat_q, lined_q),
            jnp.dot(coarse_factor.T, rhs_r, precision=exact_mode),
            jnp.dot(coarse_factor.T, rhs_q, precision=exact_mode),
        ),
        ("sub", "inner"),
    )
    gram_pq, proj_pr, image_lined_r, image_lined_q, mid_r, mid_q = summed
    lower = jnp.linalg.cholesky(gram_pq)
    alpha_mix = spd_solve(lower, proj_pr)
    flat_new = flat_r - jnp.dot(alpha_mix.T, flat_q, precision=exact_mode)
    local_part = lined_r - jnp.dot(alpha_mix.T, lined_q, precision=exact_mode)
    coarse_mid = mid_r - jnp.dot(mid_q, alpha_mix, precision=exact_mode)
    coarse_sol = jnp.dot(coarse_factor, coarse_mid, precision=exact_mode)
    precond = local_part + jnp.dot(coarse_sol.T, basis_flat, precision=exact_mode)
    cross_qz = (
        image_lined_r
        - jnp.dot(image_lined_q, alpha_mix, precision=exact_mode)
        + jnp.dot(mid_q.T, coarse_mid, precision=exact_mode)
    )
    new_solution = flat_s + jnp.dot(alpha_mix.T, flat_p, precision=exact_mode)
    beta_mix = -spd_solve(lower, cross_qz)
    new_direction = precond + jnp.dot(beta_mix.T, flat_p, precision=exact_mode)
    return (new_solution.reshape(shape), flat_new.reshape(shape), new_direction.reshape(shape))


def solution(mesh):
    placed = (
        P(None, None, "sub", "inner", None),
        P(None, None, "sub", "inner", None),
        P(None, None, "sub", "inner", None),
        P("sub", "inner", None),
        P(None, None, "sub", "inner", None),
        P("sub", "inner", None, None),
        P(("sub", "inner"), None),
    )
    return jax.shard_map(
        on_device,
        mesh=mesh,
        in_specs=placed,
        out_specs=(
            P(None, None, "sub", "inner", None),
            P(None, None, "sub", "inner", None),
            P(None, None, "sub", "inner", None),
        ),
        check_vma=False,
    )
```

profile of v0, /device:TPU:0, one launch (start us, length us, event | category | flops | bytes accessed | tf_op | source)
XLA Modules:
  0.0 269.1 jit_solution(2169634670247983347)
XLA Ops:
  8.6 1.3 collective-permute-start
  10.7 6.4 %collective-permute-start.1 = (f32[32,3,2,4,128]{4,0,3,2,1:T(8,128)}, f32[32,3,2,4,128]{4,0,3,2,1:T(8,128)}, u32[]{:S(2)}, u32[]{:S(2)}) collective-permute-start(f32[32,3,2,4,128]{4,0,3,2,1:T(8,128)} %copy.83), channel_id=1, source_target_pairs={{0,4},{4,8},{8,12},{12,16},{16,20},{20,24},{24,28},{1,5},{5,9},{9,... | collective-permute-start | bytes 1179656 | tf_op jit(solution)/shard_map/ppermute | solution.py:16
  17.1 1.3 copy.42
  18.5 2.4 reshape.56
  22.9 8.4 %collective-permute-done.1 = f32[32,3,2,4,128]{4,0,3,2,1:T(8,128)} collective-permute-done((f32[32,3,2,4,128]{4,0,3,2,1:T(8,128)}, f32[32,3,2,4,128]{4,0,3,2,1:T(8,128)}, u32[]{:S(2)}, u32[]{:S(2)}) %collective-permute-start.1) | collective-permute-done | bytes 393248 | tf_op jit(solution)/shard_map/ppermute | solution.py:16
  31.3 1.3 copy.47
  35.9 3.9 %collective-permute-start.3 = (f32[32,3,8,2,128]{4,2,3,1,0:T(8,128)}, f32[32,3,8,2,128]{4,2,3,1,0:T(8,128)}, u32[]{:S(2)}, u32[]{:S(2)}) collective-permute-start(f32[32,3,8,2,128]{4,2,3,1,0:T(8,128)} %get-tuple-element.11), channel_id=1, source_target_pairs={{0,1},{1,2},{2,3},{4,5},{5,6},{6,7},{8,9},{9,10},{10,11},{12,13},{... | collective-permute-start | bytes 2359304 | tf_op jit(solution)/shard_map/ppermute | solution.py:16
  39.8 1.7 fusion.23
  41.5 2.1 reshape.61
  44.9 2.4 reshape.55
  50.6 6.0 %select_maximum_fusion = f32[32,3,8,8,132]{4,2,3,1,0:T(8,128)S(1)} fusion(f32[32,3,8,2,128]{4,2,3,1,0:T(8,128)} %collective-permute-done.2, f32[32,3,8,2,128]{4,2,3,1,0:T(8,128)} %collective-permute-done.3, f32[32,3,2,4,128]{4,2,3,1,0:T(2,128)} %copy-done.5, f32[32,3,4,4,128]{4,2,3,1,0:T(4,128)S(1)} %copy.42, f32[32,3,2,4,128]{4,2,3,1,0:T(2,128)} %copy-done.7), kind=kLoop, calls=%fused_computation.7 | loop fusion | flops 9732096 | bytes 6389760 | tf_op jit(solution)/shard_map/concatenate | solution.py:18
  56.7 5.1 %fusion.9 = f32[32,3,4,4,128]{4,2,3,1,0:T(4,128)S(1)} fusion(f32[32,3,2,4,128]{4,2,3,1,0:T(2,128)S(1)} %copy-done.8, f32[32,3,4,4,128]{4,2,3,1,0:T(4,128)S(1)} %copy.42, f32[32,3,2,4,128]{4,2,3,1,0:T(2,128)S(1)} %copy-done.6, f32[32,3,8,8,132]{4,2,3,1,0:T(8,128)S(1)} %select_maximum_fusion, f32[32,3,8,2,128]{4,2,3,1,0:T(8,128)} %collective-permute-done.3, ...), kind=kLoop, calls=%fused_computation.35 | loop fusion | flops 6094848 | bytes 7086080 | tf_op jit(solution)/shard_map/add | solution.py:42
  66.4 1.9 fusion.39
  68.3 42.4 %all-reduce.1 = (f32[32,32]{1,0:T(8,128)S(1)}, f32[32,32]{0,1:T(8,128)S(1)}, f32[32,32]{1,0:T(8,128)S(1)}, f32[32,32]{1,0:T(8,128)S(1)}) all-reduce(f32[32,32]{1,0:T(8,128)S(1)} %convolution_bitcast_fusion.4, f32[32,32]{0,1:T(8,128)S(1)} %convolution_bitcast_fusion.5, ...), channel_id=1, replica_groups=mesh['sub'=8,'inner'=4] {'sub','inner'}, use_global_device_ids=true, to_apply=%region_3.4 | all-reduce | flops 4096 | bytes 32768 | tf_op jit(solution)/shard_map/psum | solution.py:73
  110.8 2.9 %cholesky.18 = f32[32,32]{1,0:T(8,128)S(1)} custom-call(f32[32,32]{1,0:T(8,128)S(1)} %fusion.33), custom_call_target="Cholesky" | custom-call | tf_op jit(solution)/shard_map/jit(cholesky)/cholesky | solution.py:85
  115.0 2.4 custom-call.12
  118.8 2.8 %convolution_subtract_fusion = f32[32,6144]{1,0:T(8,128)} fusion(f32[32,6144]{1,0:T(8,128)} %reshape.61, f32[32,32]{1,0:T(8,128)S(1)} %fusion.31, f32[32,6144]{1,0:T(8,128)S(1)} %reshape.62), kind=kOutput, calls=%fused_computation.4 | convolution fusion | flops 75694080 | bytes 2363392 | tf_op jit(solution)/shard_map/dot_general | solution.py:88
  121.6 2.0 convolution_subtract_fusion.1
  123.6 1.4 reshape.60
  125.0 1.9 convolution_add_fusion.2
  126.9 1.4 reshape.57
  128.5 126.6 %all-reduce.5.cloned.1.call-done = (f32[1024,32]{0,1:T(8,128)}, f32[1024,32]{0,1:T(8,128)}) async-done(((f32[1024,32]{0,1:T(8,128)}, f32[1024,32]{0,1:T(8,128)}), (f32[1024,32]{0,1:T(8,128)}, f32[1024,32]{0,1:T(8,128)})) %all-reduce.5.cloned.1.call-update) | async-done | bytes 262160 | tf_op jit(solution)/shard_map/psum | solution.py:73
  258.1 1.9 convolution_add_fusion.1
  260.9 1.4 reshape.64
  (65 shorter events, 23.4 us)
Async XLA Ops:
  7.2 42.4 %copy-start = (f32[32,1024]{1,0:T(8,128)S(1)}, f32[32,1024]{1,0:T(8,128)}, u32[]{:S(2)}) copy-start(f32[32,1024]{1,0:T(8,128)} %param.17) | copy-start | bytes 393220
  7.2 13.7 %copy-start.11 = (f32[4,4,128]{2,1,0:T(4,128)S(1)}, f32[4,4,128]{2,1,0:T(4,128)}, u32[]{:S(2)}) copy-start(f32[4,4,128]{2,1,0:T(4,128)} %param.14) | copy-start | bytes 24580
  7.2 13.7 %copy-start.2 = (f32[32,3,4,4,128]{4,3,2,1,0:T(4,128)S(1)}, f32[32,3,4,4,128]{4,3,2,1,0:T(4,128)}, u32[]{:S(2)}) copy-start(f32[32,3,4,4,128]{4,3,2,1,0:T(4,128)} %param.12) | copy-start | bytes 2359300
  7.2 247.9 %all-reduce.5.cloned.1.call-start = ((), (), s32[]{:S(2)}) async-start(), calls=%async_computation | async-start | bytes 524288 | tf_op jit(solution)/shard_map/psum | solution.py:73
  8.6 14.0 %collective-permute-start = (f32[32,3,2,4,128]{4,0,3,2,1:T(8,128)S(1)}, f32[32,3,2,4,128]{4,0,3,2,1:T(8,128)S(1)}, u32[]{:S(2)}, u32[]{:S(2)}) collective-permute-start(f32[32,3,2,4,128]{4,0,3,2,1:T(8,128)S(1)} %copy.84), channel_id=1, source_target_pairs={{4,0},{8,4},{12,8},{16,12},{20,16},{24,20},{28,24},{5,1},{9,5},{13... | collective-permute-start | bytes 1179656 | tf_op jit(solution)/shard_map/ppermute | solution.py:17
  10.7 29.1 %copy-start.10 = (f32[1,1,128,128]{3,2,1,0:T(8,128)S(1)}, f32[1,1,128,128]{3,2,1,0:T(8,128)}, u32[]{:S(2)}) copy-start(f32[1,1,128,128]{3,2,1,0:T(8,128)} %param.16) | copy-start | bytes 196612
  10.7 20.6 %collective-permute-start.1 = (f32[32,3,2,4,128]{4,0,3,2,1:T(8,128)}, f32[32,3,2,4,128]{4,0,3,2,1:T(8,128)}, u32[]{:S(2)}, u32[]{:S(2)}) collective-permute-start(f32[32,3,2,4,128]{4,0,3,2,1:T(8,128)} %copy.83), channel_id=1, source_target_pairs={{0,4},{4,8},{8,12},{12,16},{16,20},{20,24},{24,28},{1,5},{5,9},{9,... | collective-permute-start | bytes 1179656 | tf_op jit(solution)/shard_map/ppermute | solution.py:16
  20.9 22.8 %copy-start.3 = (f32[32,3,4,4,128]{4,3,2,1,0:T(4,128)S(1)}, f32[32,3,4,4,128]{4,3,2,1,0:T(4,128)}, u32[]{:S(2)}) copy-start(f32[32,3,4,4,128]{4,3,2,1,0:T(4,128)} %param.15) | copy-start | bytes 2359300
  22.9 9.7 %copy-start.5 = (f32[32,3,2,4,128]{4,2,3,1,0:T(2,128)}, f32[32,3,2,4,128]{4,2,3,1,0:T(2,128)S(1)}, u32[]{:S(2)}) copy-start(f32[32,3,2,4,128]{4,2,3,1,0:T(2,128)S(1)} %copy.45) | copy-start | bytes 1179652
  32.6 0.8 copy-start.7
  32.6 14.6 %copy-start.1 = (f32[32,3,4,4,128]{4,3,2,1,0:T(4,128)S(1)}, f32[32,3,4,4,128]{4,3,2,1,0:T(4,128)}, u32[]{:S(2)}) copy-start(f32[32,3,4,4,128]{4,3,2,1,0:T(4,128)} %param.13) | copy-start | bytes 2359300
  34.6 16.0 %collective-permute-start.2 = (f32[32,3,8,2,128]{4,2,3,1,0:T(8,128)}, f32[32,3,8,2,128]{4,2,3,1,0:T(8,128)}, u32[]{:S(2)}, u32[]{:S(2)}) collective-permute-start(f32[32,3,8,2,128]{4,2,3,1,0:T(8,128)} %get-tuple-element.12), channel_id=1, source_target_pairs={{1,0},{2,1},{3,2},{5,4},{6,5},{7,6},{9,8},{10,9},{11,10},{13,12},{... | collective-permute-start | bytes 2359304 | tf_op jit(solution)/shard_map/ppermute | solution.py:17
  35.9 14.7 %collective-permute-start.3 = (f32[32,3,8,2,128]{4,2,3,1,0:T(8,128)}, f32[32,3,8,2,128]{4,2,3,1,0:T(8,128)}, u32[]{:S(2)}, u32[]{:S(2)}) collective-permute-start(f32[32,3,8,2,128]{4,2,3,1,0:T(8,128)} %get-tuple-element.11), channel_id=1, source_target_pairs={{0,1},{1,2},{2,3},{4,5},{5,6},{6,7},{8,9},{9,10},{10,11},{12,13},{... | collective-permute-start | bytes 2359304 | tf_op jit(solution)/shard_map/ppermute | solution.py:16
  47.3 9.4 %copy-start.6 = (f32[32,3,2,4,128]{4,2,3,1,0:T(2,128)S(1)}, f32[32,3,2,4,128]{4,2,3,1,0:T(2,128)}, u32[]{:S(2)}) copy-start(f32[32,3,2,4,128]{4,2,3,1,0:T(2,128)} %copy-done.5) | copy-start | bytes 1179652
  47.3 9.4 %copy-start.8 = (f32[32,3,2,4,128]{4,2,3,1,0:T(2,128)S(1)}, f32[32,3,2,4,128]{4,2,3,1,0:T(2,128)}, u32[]{:S(2)}) copy-start(f32[32,3,2,4,128]{4,2,3,1,0:T(2,128)} %copy-done.7) | copy-start | bytes 1179652
  64.7 60.3 %copy-start.4 = (f32[32,6144]{1,0:T(8,128)S(1)}, f32[32,6144]{1,0:T(8,128)}, u32[]{:S(2)}) copy-start(f32[32,6144]{1,0:T(8,128)} %reshape.56) | copy-start | bytes 2359300
  68.3 189.8 %copy-start.9 = (f32[32,6144]{1,0:T(8,128)S(1)}, f32[32,6144]{1,0:T(8,128)}, u32[]{:S(2)}) copy-start(f32[32,6144]{1,0:T(8,128)} %reshape.63) | copy-start | bytes 2359300
Sparse Core Ops, SparseCore 0:
  128.5 126.5 all-reduce.4
where the time goes:
time: 270 us; the launch traced here: 269 us
  waiting for transfers between devices  135 us (50%)
  blocking collectives  42.4 us (16%)
  matrix products  24.7 us (9%)
  local copies, waits for them, and re-layouts  21 us (8%)
  other arithmetic  18.4 us (7%)
  between operations  14.4 us (5%)
  starting transfers between devices  12.9 us (5%)
    psum x1, waiting for transfers between devices, on_device(): lax.psum((product(flat_p, flat_q), product(flat_p, flat_r), product(flat_...  127 us
    psum x1, blocking collectives, on_device(): lax.psum((product(flat_p, flat_q), product(flat_p, flat_r), product(flat_...  42.4 us
    ppermute x2, starting transfers between devices, with_halo(): before = lax.ppermute(last, axis, up)  10.3 us
    ppermute x2, waiting for transfers between devices, with_halo(): before = lax.ppermute(last, axis, up)  8.37 us
    dot_general x6, matrix products, product(): return jnp.dot(left, right.T, precision=exact_mode)  7.32 us
    concatenate x2, other arithmetic, with_halo(): array = jnp.concatenate([before, array, after], axis=dim)  6.55 us
  transfers between devices with their start and end apart: 5, of which 3 were waited for; matrix products, arithmetic and copies ran while one was open for 6% of the time, Pallas kernels for 0%

commit v1 on v0

--- a/solution.py
+++ b/solution.py
@@ -1,9 +1,120 @@
+import functools
+
 import jax
 import jax.numpy as jnp
 from jax import lax
+from jax.experimental import pallas as pl
+from jax.experimental.pallas import tpu as pltpu
 from jax.sharding import PartitionSpec as P
 
 exact_mode = lax.Precision.HIGHEST
+close_mode = lax.Precision.HIGH
+
+
+def sum_kernel(stages, wide_ref, small_ref, wide_out, small_out, *scratch):
+    count = len(stages)
+    total, held, small_parts, small_landed = scratch[:4]
+    landed = scratch[4 : 4 + count]
+    send_sem, recv_sem, small_send, small_recv, back_send, back_recv = scratch[4 + count :]
+    bits, partners = ([], [])
+    for axis, stride in stages:
+        index = lax.axis_index(axis)
+        bit = (index // stride) % 2
+        bits.append(bit)
+        partners.append({axis: index + stride * (1 - 2 * bit)})
+    barrier = pltpu.get_barrier_semaphore()
+    for partner in partners:
+        pl.semaphore_signal(barrier, inc=1, device_id=partner, device_id_type=pl.DeviceIdType.MESH)
+    pl.semaphore_wait(barrier, count)
+
+    width = wide_ref.shape[0]
+    base = 0
+    for t in range(count):
+        half = width // 2
+        keep = pl.multiple_of(base + bits[t] * half, 8)
+        give = pl.multiple_of(base + (1 - bits[t]) * half, 8)
+        source = wide_ref if t == 0 else total
+        small_source = small_ref if t == 0 else small_parts.at[t - 1]
+        small_copy = pltpu.make_async_remote_copy(
+            src_ref=small_source,
+            dst_ref=small_landed.at[t],
+            send_sem=small_send.at[t],
+            recv_sem=small_recv.at[t],
+            device_id=partners[t],
+            device_id_type=pl.DeviceIdType.MESH,
+        )
+        copy = pltpu.make_async_remote_copy(
+            src_ref=source.at[pl.ds(give, half)],
+            dst_ref=landed[t],
+            send_sem=send_sem.at[t],
+            recv_sem=recv_sem.at[t],
+            device_id=partners[t],
+            device_id_type=pl.DeviceIdType.MESH,
+        )
+        small_copy.start()
+        copy.start()
+        small_copy.wait()
+        small_sum = small_source[...] + small_landed[t]
+        if t < count - 1:
+            small_parts[t] = small_sum
+        else:
+            small_out[...] = small_sum
+        copy.wait()
+        target = total if t < count - 1 else held
+        target[pl.ds(keep, half), :] = source[pl.ds(keep, half), :] + landed[t][...]
+        base = base + bits[t] * half
+        width = half
+    for t in reversed(range(count)):
+        mine = pl.ds(pl.multiple_of(base, 8), width)
+        copy = pltpu.make_async_remote_copy(
+            src_ref=held.at[mine],
+            dst_ref=held.at[mine],
+            send_sem=back_send.at[t],
+            recv_sem=back_recv.at[t],
+            device_id=partners[t],
+            device_id_type=pl.DeviceIdType.MESH,
+        )
+        copy.start()
+        copy.wait()
+        base = base - bits[t] * width
+        width = width * 2
+    wide_out[...] = held[...]
+
+
+def sum_everywhere(wide, small, axes):
+    stages = []
+    for axis in axes:
+        stride = 1
+        while stride < lax.axis_size(axis):
+            stages.append((axis, stride))
+            stride *= 2
+    count = len(stages)
+    rows, lanes = wide.shape
+    vmem = pl.BlockSpec(memory_space=pltpu.VMEM)
+    dma = pltpu.SemaphoreType.DMA((count,))
+    return pl.pallas_call(
+        functools.partial(sum_kernel, tuple(stages)),
+        out_shape=(
+            jax.ShapeDtypeStruct(wide.shape, wide.dtype),
+            jax.ShapeDtypeStruct(small.shape, small.dtype),
+        ),
+        in_specs=[vmem, vmem],
+        out_specs=(vmem, vmem),
+        scratch_shapes=[
+            pltpu.VMEM(wide.shape, wide.dtype),
+            pltpu.VMEM(wide.shape, wide.dtype),
+            pltpu.VMEM((count,) + small.shape, small.dtype),
+            pltpu.VMEM((count,) + small.shape, small.dtype),
+            *[pltpu.VMEM((rows >> (t + 1), lanes), wide.dtype) for t in range(count)],
+            dma,
+            dma,
+            dma,
+            dma,
+            dma,
+            dma,
+        ],
+        compiler_params=pltpu.CompilerParams(collective_id=0, has_side_effects=True),
+    )(wide, small)
 
 
 def with_halo(array, sides, width):
@@ -49,7 +160,7 @@
 
 def along_lines(flat, inverse):
     lines = flat.reshape(-1, inverse.shape[0])
-    return jnp.dot(lines, inverse.T, precision=exact_mode).reshape(flat.shape)
+    return jnp.dot(lines, inverse.T, precision=close_mode).reshape(flat.shape)
 
 
 def product(left, right):
@@ -70,33 +181,37 @@
     lined_q = along_lines(flat_q, inverse)
     rhs_r = product(basis_flat, flat_r)
     rhs_q = product(basis_flat, flat_q)
-    summed = lax.psum(
-        (
-            product(flat_p, flat_q),
-            product(flat_p, flat_r),
-            product(flat_q, lined_r),
-            product(flat_q, lined_q),
-            jnp.dot(coarse_factor.T, rhs_r, precision=exact_mode),
-            jnp.dot(coarse_factor.T, rhs_q, precision=exact_mode),
-        ),
-        ("sub", "inner"),
-    )
-    gram_pq, proj_pr, image_lined_r, image_lined_q, mid_r, mid_q = summed
+    small = jnp.concatenate(
+        [product(flat_p, flat_q), product(flat_p, flat_r), product(flat_q, lined_r), product(flat_q, lined_q)], axis=1
+    )
+    rhs_both = jnp.concatenate([rhs_r, rhs_q], axis=1)
+    half = coarse_factor.shape[1] // 2
+    wide = jnp.concatenate(
+        [
+            jnp.dot(coarse_factor[:, :half].T, rhs_both, precision=exact_mode),
+            jnp.dot(coarse_factor[:, half:].T, rhs_both, precision=exact_mode),
+        ],
+        axis=1,
+    )
+    wide, small = sum_everywhere(wide, small, ("inner", "sub"))
+    gram_pq, proj_pr, image_lined_r, image_lined_q = jnp.split(small, 4, axis=1)
+    mids = jnp.concatenate([wide[:, : 2 * directions], wide[:, 2 * directions :]], axis=0)
+    mid_r, mid_q = (mids[:, :directions], mids[:, directions:])
     lower = jnp.linalg.cholesky(gram_pq)
     alpha_mix = spd_solve(lower, proj_pr)
-    flat_new = flat_r - jnp.dot(alpha_mix.T, flat_q, precision=exact_mode)
-    local_part = lined_r - jnp.dot(alpha_mix.T, lined_q, precision=exact_mode)
+    flat_new = flat_r - jnp.dot(alpha_mix.T, flat_q, precision=close_mode)
+    local_part = lined_r - jnp.dot(alpha_mix.T, lined_q, precision=close_mode)
     coarse_mid = mid_r - jnp.dot(mid_q, alpha_mix, precision=exact_mode)
     coarse_sol = jnp.dot(coarse_factor, coarse_mid, precision=exact_mode)
-    precond = local_part + jnp.dot(coarse_sol.T, basis_flat, precision=exact_mode)
+    precond = local_part + jnp.dot(coarse_sol.T, basis_flat, precision=close_mode)
     cross_qz = (
         image_lined_r
         - jnp.dot(image_lined_q, alpha_mix, precision=exact_mode)
         + jnp.dot(mid_q.T, coarse_mid, precision=exact_mode)
     )
-    new_solution = flat_s + jnp.dot(alpha_mix.T, flat_p, precision=exact_mode)
+    new_solution = flat_s + jnp.dot(alpha_mix.T, flat_p, precision=close_mode)
     beta_mix = -spd_solve(lower, cross_qz)
-    new_direction = precond + jnp.dot(beta_mix.T, flat_p, precision=exact_mode)
+    new_direction = precond + jnp.dot(beta_mix.T, flat_p, precision=close_mode)
     return (new_solution.reshape(shape), flat_new.reshape(shape), new_direction.reshape(shape))
 
 

time: 270 us -> 124 us (0.46)
  waiting for transfers between devices: 135 us -> 10.3 us
  blocking collectives: 42.4 us -> 0 us
  Pallas kernels: 0 us -> 32.2 us
  between operations: 14.4 us -> 1.03 us
  local copies, waits for them, and re-layouts: 21 us -> 24.1 us
    psum x1 -> x0, waiting for transfers between devices: 127 us -> none  [on_device(): lax.psum((product(flat_p, flat_q), product(flat_p, flat_r), product(flat_...]
    psum x1 -> x0, blocking collectives: 42.4 us -> none  [on_device(): lax.psum((product(flat_p, flat_q), product(flat_p, flat_r), product(flat_...]
    pallas_call x0 -> x1, Pallas kernels: none -> 32.2 us  [sum_everywhere(): pl.pallas_call(functools.partial(sum_kernel, tuple(stages)), out_shape=(j...]
    dot_general x9, matrix products: 13.8 us -> 8.34 us  [the longest x2 2.74 us: along_lines(): return jnp.dot(lines, inverse.T, precision=close_mode).reshape(flat.shape)]
  transfers between devices with their start and end apart: 5 -> 4, of which waited for: 3 -> 2; matrix products, arithmetic and copies ran while one was open for 6% -> 13% of each run, Pallas kernels for 0% -> 0%
where the time goes in v1:
time: 124 us; the launch traced here: 123 us
  Pallas kernels  32.2 us (26%)
  local copies, waits for them, and re-layouts  24.1 us (19%)
  matrix products  22 us (18%)
  other arithmetic  20.9 us (17%)
  starting transfers between devices  12.9 us (10%)
  waiting for transfers between devices  10.3 us (8%)
    pallas_call x1, Pallas kernels, sum_everywhere(): pl.pallas_call(functools.partial(sum_kernel, tuple(stages)), out_shape=(j...  32.2 us
    ppermute x2, starting transfers between devices, with_halo(): before = lax.ppermute(last, axis, up)  10.2 us
    ppermute x2, waiting for transfers between devices, with_halo(): before = lax.ppermute(last, axis, up)  8.37 us
    dot_general x6, matrix products, product(): return jnp.dot(left, right.T, precision=exact_mode)  7.4 us
    concatenate x2, other arithmetic, with_halo(): array = jnp.concatenate([before, array, after], axis=dim)  6.37 us
    add x2, other arithmetic, operate(): return (mass + 7.5) * center - 4.0 / 3.0 * nearby + 1.0 / 12.0 * farther  5.33 us
    another operation x3, other arithmetic, on_device(): lower = jnp.linalg.cholesky(gram_pq)  3.6 us
    reshape x2, local copies, waits for them, and re-layouts, along_lines(): return jnp.dot(lines, inverse.T, precision=close_mode).reshape(flat.shape)  3.4 us
  transfers between devices with their start and end apart: 4, of which 2 were waited for; matrix products, arithmetic and copies ran while one was open for 13% of the time, Pallas kernels for 0%

profile of v1, /device:TPU:0, one launch (start us, length us, event | category | flops | bytes accessed | tf_op | source)
XLA Modules:
  0.0 123.4 jit_solution(9809226903969542695)
XLA Ops:
  2.0 1.4 %collective-permute-start = (f32[32,3,2,4,128]{4,0,3,2,1:T(8,128)S(1)}, f32[32,3,2,4,128]{4,0,3,2,1:T(8,128)S(1)}, u32[]{:S(2)}, u32[]{:S(2)}) collective-permute-start(f32[32,3,2,4,128]{4,0,3,2,1:T(8,128)S(1)} %copy.115), channel_id=1, source_target_pairs={{4,0},{8,4},{12,8},{16,12},{20,16},{24,20},{28,24},{5,1},{9,5},{13... | collective-permute-start | bytes 1179656 | tf_op jit(solution)/shard_map/ppermute | solution.py:128
  4.2 6.3 %collective-permute-start.1 = (f32[32,3,2,4,128]{4,0,3,2,1:T(8,128)}, f32[32,3,2,4,128]{4,0,3,2,1:T(8,128)}, u32[]{:S(2)}, u32[]{:S(2)}) collective-permute-start(f32[32,3,2,4,128]{4,0,3,2,1:T(8,128)} %copy.114), channel_id=1, source_target_pairs={{0,4},{4,8},{8,12},{12,16},{16,20},{20,24},{24,28},{1,5},{5,9},{9,... | collective-permute-start | bytes 1179656 | tf_op jit(solution)/shard_map/ppermute | solution.py:127
  10.5 1.3 %copy.68 = f32[32,3,4,4,128]{4,2,3,1,0:T(4,128)S(1)} copy(f32[32,3,4,4,128]{4,3,2,1,0:T(4,128)} %param.13) | data formatting | bytes 1572864 | tf_op args[2]
  11.9 2.4 %reshape.59 = f32[32,6144]{1,0:T(8,128)} reshape(f32[32,3,4,4,128]{4,3,2,1,0:T(4,128)} %param.13) | data formatting | bytes 1572864 | tf_op jit(solution)/shard_map/reshape | solution.py:175
  14.2 1.9 %collective-permute-done = f32[32,3,2,4,128]{4,0,3,2,1:T(8,128)S(1)} collective-permute-done((f32[32,3,2,4,128]{4,0,3,2,1:T(8,128)S(1)}, f32[32,3,2,4,128]{4,0,3,2,1:T(8,128)S(1)}, u32[]{:S(2)}, u32[]{:S(2)}) %collective-permute-start) | collective-permute-done | bytes 393248 | tf_op jit(solution)/shard_map/ppermute | solution.py:128
  16.4 8.4 %collective-permute-done.1 = f32[32,3,2,4,128]{4,0,3,2,1:T(8,128)} collective-permute-done((f32[32,3,2,4,128]{4,0,3,2,1:T(8,128)}, f32[32,3,2,4,128]{4,0,3,2,1:T(8,128)}, u32[]{:S(2)}, u32[]{:S(2)}) %collective-permute-start.1) | collective-permute-done | bytes 393248 | tf_op jit(solution)/shard_map/ppermute | solution.py:127
  29.4 3.9 %collective-permute-start.3 = (f32[32,3,8,2,128]{4,2,3,1,0:T(8,128)}, f32[32,3,8,2,128]{4,2,3,1,0:T(8,128)}, u32[]{:S(2)}, u32[]{:S(2)}) collective-permute-start(f32[32,3,8,2,128]{4,2,3,1,0:T(8,128)} %get-tuple-element.9), channel_id=1, source_target_pairs={{0,1},{1,2},{2,3},{4,5},{5,6},{6,7},{8,9},{9,10},{10,11},{12,13},{... | collective-permute-start | bytes 2359304 | tf_op jit(solution)/shard_map/ppermute | solution.py:127
  34.7 1.4 %fusion.23 = f32[1536,128]{1,0:T(8,128)} fusion(f32[1536,128]{1,0:T(8,128)S(1)} %bitcast.76, f32[1,1,128,128]{3,2,1,0:T(8,128)S(1)} %copy-done), kind=kOutput, calls=%fused_computation.61 | convolution fusion | flops 150994944 | bytes 1638400 | tf_op jit(solution)/shard_map/dot_general | solution.py:163
  36.0 2.1 %reshape.57 = f32[32,6144]{1,0:T(8,128)} reshape(f32[1536,128]{1,0:T(8,128)} %fusion.23) | data formatting | bytes 1572864 | tf_op jit(solution)/shard_map/reshape | solution.py:163
  39.4 2.4 %reshape.55 = f32[32,6144]{1,0:T(8,128)} reshape(f32[32,3,4,4,128]{4,3,2,1,0:T(4,128)} %param.11) | data formatting | bytes 1572864 | tf_op jit(solution)/shard_map/reshape | solution.py:178
  44.1 5.9 %select_maximum_fusion = f32[32,3,8,8,132]{4,2,3,1,0:T(8,128)S(1)} fusion(f32[32,3,8,2,128]{4,2,3,1,0:T(8,128)} %collective-permute-done.2, f32[32,3,8,2,128]{4,2,3,1,0:T(8,128)} %collective-permute-done.3, f32[32,3,2,4,128]{4,2,3,1,0:T(2,128)} %copy-done.6, f32[32,3,4,4,128]{4,2,3,1,0:T(4,128)S(1)} %copy.68, f32[32,3,2,4,128]{4,2,3,1,0:T(2,128)} %copy-done.8), kind=kLoop, calls=%fused_computation.7 | loop fusion | flops 9732096 | bytes 6389760 | tf_op jit(solution)/shard_map/concatenate | solution.py:129
  50.0 5.3 %fusion.9 = f32[32,3,4,4,128]{4,2,3,1,0:T(4,128)S(1)} fusion(f32[32,3,2,4,128]{4,2,3,1,0:T(2,128)S(1)} %copy-done.9, f32[32,3,4,4,128]{4,2,3,1,0:T(4,128)S(1)} %copy.68, f32[32,3,2,4,128]{4,2,3,1,0:T(2,128)S(1)} %copy-done.7, f32[32,3,8,8,132]{4,2,3,1,0:T(8,128)S(1)} %select_maximum_fusion, f32[32,3,8,2,128]{4,2,3,1,0:T(8,128)} %collective-permute-done.3, ...), kind=kLoop, calls=%fused_computation.35 | loop fusion | flops 6094848 | bytes 7086080 | tf_op jit(solution)/shard_map/add | solution.py:153
  58.6 1.3 %convolution_bitcast_fusion.1 = f32[512,64]{1,0:T(8,128)} fusion(f32[32,1024]{1,0:T(8,128)S(1)} %copy-done.12, f32[32,32]{1,0:T(8,128)S(1)} %convolution_bitcast_fusion.4, f32[32,32]{1,0:T(8,128)S(1)} %convolution_bitcast_fusion.5), kind=kOutput, calls=%fused_computation.19 | convolution fusion | flops 12584960 | bytes 229376 | tf_op jit(solution)/shard_map/dot_general | solution.py:191
  60.3 1.4 %fusion.21 = f32[1536,128]{1,0:T(8,128)} fusion(f32[1536,128]{1,0:T(8,128)S(1)} %bitcast.77, f32[1,1,128,128]{3,2,1,0:T(8,128)S(1)} %copy-done), kind=kOutput, calls=%fused_computation.59 | convolution fusion | flops 150994944 | bytes 1638400 | tf_op jit(solution)/shard_map/dot_general | solution.py:163
  63.7 2.0 %fusion.47 = f32[32,32]{1,0:T(8,128)S(1)} fusion(f32[32,6144]{1,0:T(8,128)S(1)} %reshape.56, f32[32,6144]{1,0:T(8,128)} %reshape.57), kind=kOutput, calls=%fused_computation.94 | convolution fusion | flops 75497472 | bytes 1576960 | tf_op jit(solution)/shard_map/dot_general | solution.py:167
  65.6 1.8 %pad_maximum_fusion.12.wide_ref = f32[512,128]{1,0:T(8,128)} fusion(f32[512,64]{1,0:T(8,128)S(1)} %convolution_bitcast_fusion, f32[512,64]{1,0:T(8,128)} %convolution_bitcast_fusion.1), kind=kLoop, calls=%fused_computation.58 | loop fusion | flops 65536 | bytes 524288 | tf_op jit(solution)/shard_map/concatenate | solution.py:189
  68.1 32.2 %shard_map.94 = (f32[512,128]{1,0:T(8,128)}, f32[32,128]{1,0:T(8,128)}) custom-call(f32[512,128]{1,0:T(8,128)} %pad_maximum_fusion.12.wide_ref, f32[32,128]{1,0:T(8,128)} %pad_maximum_fusion.14.small_ref), custom_call_target="tpu_custom_call" | custom-call | tf_op jit(solution)/shard_map/pallas_call | solution.py:95
  101.2 2.9 %cholesky.18 = f32[32,32]{1,0:T(8,128)S(1)} custom-call(f32[32,32]{1,0:T(8,128)S(1)} %fusion.35), custom_call_target="Cholesky" | custom-call | tf_op jit(solution)/shard_map/jit(cholesky)/cholesky | solution.py:200
  105.5 2.4 %custom-call.12 = f32[1,32,32]{1,2,0:T(8,128)S(1)} custom-call(f32[1,32,32]{2,1,0:T(8,128)S(1)} %fusion.27), custom_call_target="InvertDiagBlocksLowerTriangular" | custom-call | tf_op jit(solution)/shard_map/triangular_solve/custom-call.2 | solution.py:158
  112.5 1.9 %fusion.49 = f32[32,32]{1,0:T(8,128)S(1)} fusion(f32[1024,32]{1,0:T(8,128)S(1)} %convolution_subtract_fusion.2, f32[32,1024]{1,0:T(8,128)} %param.17), kind=kOutput, calls=%fused_computation.96 | convolution fusion | flops 12582912 | bytes 266240 | tf_op jit(solution)/shard_map/dot_general | solution.py:205
  117.0 1.4 %reshape.64 = f32[32,3,4,4,128]{4,3,2,1,0:T(4,128)} reshape(f32[32,6144]{1,0:T(8,128)S(1)} %convolution_add_fusion) | data formatting | bytes 1572864 | tf_op jit(solution)/shard_map/reshape | solution.py:215
  118.4 1.6 %convolution_subtract_fusion.1 = f32[32,6144]{1,0:T(8,128)S(1)} fusion(f32[32,6144]{1,0:T(8,128)} %reshape.61, f32[32,32]{1,0:T(8,128)S(1)} %fusion.33, f32[32,6144]{1,0:T(8,128)S(1)} %reshape.56), kind=kOutput, calls=%fused_computation.5 | convolution fusion | flops 37945344 | bytes 2363392 | tf_op jit(solution)/shard_map/dot_general | solution.py:202
  120.0 1.4 %reshape.62 = f32[32,3,4,4,128]{4,3,2,1,0:T(4,128)} reshape(f32[32,6144]{1,0:T(8,128)S(1)} %convolution_subtract_fusion.1) | data formatting | bytes 1572864 | tf_op jit(solution)/shard_map/reshape | solution.py:215
  122.0 1.4 %reshape.60 = f32[32,3,4,4,128]{4,3,2,1,0:T(4,128)} reshape(f32[32,6144]{1,0:T(8,128)S(1)} %convolution_add_fusion.2) | data formatting | bytes 1572864 | tf_op jit(solution)/shard_map/reshape | solution.py:215
  (71 shorter events, 27.9 us)
Async XLA Ops:
  0.6 34.0 %copy-start = (f32[1,1,128,128]{3,2,1,0:T(8,128)S(1)}, f32[1,1,128,128]{3,2,1,0:T(8,128)}, u32[]{:S(2)}) copy-start(f32[1,1,128,128]{3,2,1,0:T(8,128)} %param.16) | copy-start | bytes 196612
  1.9 31.5 %copy-start.13 = (f32[4,4,128]{2,1,0:T(4,128)S(1)}, f32[4,4,128]{2,1,0:T(4,128)}, u32[]{:S(2)}) copy-start(f32[4,4,128]{2,1,0:T(4,128)} %param.14) | copy-start | bytes 24580
  1.9 31.5 %copy-start.2 = (f32[32,3,4,4,128]{4,3,2,1,0:T(4,128)S(1)}, f32[32,3,4,4,128]{4,3,2,1,0:T(4,128)}, u32[]{:S(2)}) copy-start(f32[32,3,4,4,128]{4,3,2,1,0:T(4,128)} %param.12) | copy-start | bytes 2359300
  2.0 14.1 %collective-permute-start = (f32[32,3,2,4,128]{4,0,3,2,1:T(8,128)S(1)}, f32[32,3,2,4,128]{4,0,3,2,1:T(8,128)S(1)}, u32[]{:S(2)}, u32[]{:S(2)}) collective-permute-start(f32[32,3,2,4,128]{4,0,3,2,1:T(8,128)S(1)} %copy.115), channel_id=1, source_target_pairs={{4,0},{8,4},{12,8},{16,12},{20,16},{24,20},{28,24},{5,1},{9,5},{13... | collective-permute-start | bytes 1179656 | tf_op jit(solution)/shard_map/ppermute | solution.py:128
  4.2 20.6 %collective-permute-start.1 = (f32[32,3,2,4,128]{4,0,3,2,1:T(8,128)}, f32[32,3,2,4,128]{4,0,3,2,1:T(8,128)}, u32[]{:S(2)}, u32[]{:S(2)}) collective-permute-start(f32[32,3,2,4,128]{4,0,3,2,1:T(8,128)} %copy.114), channel_id=1, source_target_pairs={{0,4},{4,8},{8,12},{12,16},{16,20},{20,24},{24,28},{1,5},{5,9},{9,... | collective-permute-start | bytes 1179656 | tf_op jit(solution)/shard_map/ppermute | solution.py:127
  14.2 23.9 %copy-start.3 = (f32[32,3,4,4,128]{4,3,2,1,0:T(4,128)S(1)}, f32[32,3,4,4,128]{4,3,2,1,0:T(4,128)}, u32[]{:S(2)}) copy-start(f32[32,3,4,4,128]{4,3,2,1,0:T(4,128)} %param.15) | copy-start | bytes 2359300
  16.4 9.7 %copy-start.6 = (f32[32,3,2,4,128]{4,2,3,1,0:T(2,128)}, f32[32,3,2,4,128]{4,2,3,1,0:T(2,128)S(1)}, u32[]{:S(2)}) copy-start(f32[32,3,2,4,128]{4,2,3,1,0:T(2,128)S(1)} %copy.71) | copy-start | bytes 1179652
  26.1 0.8 copy-start.8
  26.9 14.9 %copy-start.1 = (f32[32,3,4,4,128]{4,3,2,1,0:T(4,128)S(1)}, f32[32,3,4,4,128]{4,3,2,1,0:T(4,128)}, u32[]{:S(2)}) copy-start(f32[32,3,4,4,128]{4,3,2,1,0:T(4,128)} %param.13) | copy-start | bytes 2359300
  28.1 16.0 %collective-permute-start.2 = (f32[32,3,8,2,128]{4,2,3,1,0:T(8,128)}, f32[32,3,8,2,128]{4,2,3,1,0:T(8,128)}, u32[]{:S(2)}, u32[]{:S(2)}) collective-permute-start(f32[32,3,8,2,128]{4,2,3,1,0:T(8,128)} %get-tuple-element.10), channel_id=1, source_target_pairs={{1,0},{2,1},{3,2},{5,4},{6,5},{7,6},{9,8},{10,9},{11,10},{13,12},{... | collective-permute-start | bytes 2359304 | tf_op jit(solution)/shard_map/ppermute | solution.py:128
  29.4 14.7 %collective-permute-start.3 = (f32[32,3,8,2,128]{4,2,3,1,0:T(8,128)}, f32[32,3,8,2,128]{4,2,3,1,0:T(8,128)}, u32[]{:S(2)}, u32[]{:S(2)}) collective-permute-start(f32[32,3,8,2,128]{4,2,3,1,0:T(8,128)} %get-tuple-element.9), channel_id=1, source_target_pairs={{0,1},{1,2},{2,3},{4,5},{5,6},{6,7},{8,9},{9,10},{10,11},{12,13},{... | collective-permute-start | bytes 2359304 | tf_op jit(solution)/shard_map/ppermute | solution.py:127
  41.8 8.2 %copy-start.7 = (f32[32,3,2,4,128]{4,2,3,1,0:T(2,128)S(1)}, f32[32,3,2,4,128]{4,2,3,1,0:T(2,128)}, u32[]{:S(2)}) copy-start(f32[32,3,2,4,128]{4,2,3,1,0:T(2,128)} %copy-done.6) | copy-start | bytes 1179652
  41.8 8.2 %copy-start.9 = (f32[32,3,2,4,128]{4,2,3,1,0:T(2,128)S(1)}, f32[32,3,2,4,128]{4,2,3,1,0:T(2,128)}, u32[]{:S(2)}) copy-start(f32[32,3,2,4,128]{4,2,3,1,0:T(2,128)} %copy-done.8) | copy-start | bytes 1179652
  50.0 7.9 %copy-start.12 = (f32[32,1024]{1,0:T(8,128)S(1)}, f32[32,1024]{1,0:T(8,128)}, u32[]{:S(2)}) copy-start(f32[32,1024]{1,0:T(8,128)} %param.17) | copy-start | bytes 393220
  56.8 53.4 %copy-start.4 = (f32[32,6144]{1,0:T(8,128)S(1)}, f32[32,6144]{1,0:T(8,128)}, u32[]{:S(2)}) copy-start(f32[32,6144]{1,0:T(8,128)} %reshape.57) | copy-start | bytes 2359300
  63.7 52.8 %copy-start.5 = (f32[32,6144]{1,0:T(8,128)S(1)}, f32[32,6144]{1,0:T(8,128)}, u32[]{:S(2)}) copy-start(f32[32,6144]{1,0:T(8,128)} %reshape.59) | copy-start | bytes 2359300
  107.9 8.1 %copy-start.11 = (f32[32,6144]{1,0:T(8,128)S(1)}, f32[32,6144]{1,0:T(8,128)}, u32[]{:S(2)}) copy-start(f32[32,6144]{1,0:T(8,128)} %reshape.63) | copy-start | bytes 2359300
  112.5 9.0 %copy-start.10 = (f32[32,6144]{1,0:T(8,128)S(1)}, f32[32,6144]{1,0:T(8,128)}, u32[]{:S(2)}) copy-start(f32[32,6144]{1,0:T(8,128)} %reshape.55) | copy-start | bytes 2359300
